TPU v7x, 32 devices: a whole 2x2x4 slice. The times are simulated.
32 devices in a mesh: blk: 16 (over z, y, x), band: 2 (over core).
Axes of the slice: x: 2, y: 2, z: 4, core: 2. Of those that a mesh axis runs over, the one named last changes fastest.
Arguments:
- disp_fwd: float32 [16, 2, 25, 2048], P('blk', 'band'), may hold values from -6 to 6
- prev_fwd: float32 [16, 2, 25, 2048], P('blk', 'band'), may hold values from -6 to 6
- disp_adj: float32 [16, 2, 25, 2048], P('blk', 'band'), may hold values from -6 to 6
- prev_adj: float32 [16, 2, 25, 2048], P('blk', 'band'), may hold values from -6 to 6
- modulus: float32 [16, 2, 25, 2048], P('blk', 'band'), may hold values from 0.5 to 2
- radius: float32 [16, 2, 25], P('blk', 'band'), may hold values from 256 to 2048
- step_scale: float32 [16, 2, 25], P('blk', 'band'), may hold values from 0.01 to 0.04
- kernel_in: float32 [16, 2, 25, 2048], P('blk', 'band'), may hold values from -6 to 6
- buckets: int32 [16, 2], P('blk', 'band'), may hold values from 0 to 3
- halo_count: int32 [16, 2, 4], P('blk', 'band'), may hold values from 0 to 8, as said below
- blk_nodes: int32 [16, 2, 2, 8], P('blk', 'band'), may hold values from 0 to 24, as said below
- band_nodes: int32 [16, 2, 2, 4], P('blk', 'band'), may hold values from 0 to 24, as said below
Outputs:
- next_fwd: float32 [16, 2, 25, 2048], P('blk', 'band')
- next_adj: float32 [16, 2, 25, 2048], P('blk', 'band')
- kernel_out: float32 [16, 2, 25, 2048], P('blk', 'band')
Inputs may be any that keep to these rules, and one draw needn't show every extreme that they name: `halo_count`: entries 0 and 1 count the nodes shared with the blk neighbour below and above, entries 2 and 3 with the band neighbour below and above. A device's count toward a neighbour equals the neighbour's count back; counts toward the outside of the grid are zero; some pair along blk shares 8 nodes and some pair along band 4. Slot k of a device's list toward a blk neighbour and slot k of that neighbour's list back hold copies of one node; slots at or past the count are unused. The 24 ids of one device over blk_nodes and band_nodes are all different. `band_nodes`: slot k of a device's list toward a band neighbour and slot k of that neighbour's list back hold copies of one node; slots at or past the count are unused; ids are different from those of blk_nodes on the same device.
All inputs are finite; a program needn't handle non-finite values.
Results may differ from a plain program's by a relative error of at most 0.0046.
Values sent between devices are 32-bit elements; how exact they have to be, the bound alone decides.
A program may use at most 64 MiB of HBM per device.

v0:
```python
from functools import partial
import math

import jax
import jax.numpy as jnp
import numpy as np
from jax import lax
from jax.sharding import PartitionSpec as P


def shifted(value, axis, steps):
    count = lax.axis_size(axis)
    initial, last = (max(0, -steps), min(count, count - steps))
    return lax.ppermute(value, axis, [(source, source + steps) for source in range(initial, last)])


def gll_tables():
    inner_root = math.sqrt(3.0 / 7.0)
    points = np.array([-1.0, -inner_root, 0.0, inner_root, 1.0])
    weights = np.array([0.1, 49.0 / 90.0, 32.0 / 45.0, 49.0 / 90.0, 0.1])
    legendre = (35.0 * points**4 - 30.0 * points**2 + 3.0) / 8.0
    derivative = np.zeros((5, 5))
    for target in range(5):
        for source in range(5):
            if target != source:
                derivative[target, source] = (
                    legendre[target] / legendre[source] / (points[target] - points[source])
                )
    derivative[0, 0] = -5.0
    derivative[4, 4] = 5.0
    return (
        jnp.asarray(derivative, jnp.float32),
        jnp.asarray(np.outer(weights, weights), jnp.float32),
    )


def azimuth_table(mode_total):
    sample_len = 2 * mode_total
    table_shape = (2 * mode_total, sample_len)
    row_ids = lax.broadcasted_iota(jnp.int32, table_shape, 0)
    col_ids = lax.broadcasted_iota(jnp.int32, table_shape, 1)
    quarter = (row_ids >= mode_total).astype(jnp.int32) * (sample_len // 4)
    phase = (row_ids % mode_total * col_ids + quarter) % sample_len
    factor = math.sqrt(2.0 / sample_len)
    return (jnp.cos(phase.astype(jnp.float32) * (2.0 * math.pi / sample_len)) * factor).astype(
        jnp.bfloat16
    )


def mode_tops(mode_total):
    return [max(mode_total // 64, 1), max(mode_total // 16, 1), max(mode_total // 4, 1), mode_total]


def mode_mask(buckets, mode_total):
    order_tops = mode_tops(mode_total)
    order_limit = jnp.where(
        buckets == 0,
        order_tops[0],
        jnp.where(
            buckets == 1, order_tops[1], jnp.where(buckets == 2, order_tops[2], order_tops[3])
        ),
    )
    kept = (jnp.arange(mode_total, dtype=jnp.int32) < order_limit[..., None]).astype(jnp.float32)
    return jnp.concatenate([kept, kept], axis=-1)


def spin(coeffs, inv_radius, mode_orders):
    half_len = mode_orders.shape[0]
    return (
        jnp.concatenate(
            [-mode_orders * coeffs[..., half_len:], mode_orders * coeffs[..., :half_len]], axis=-1
        )
        * inv_radius
    )


def unspin(coeffs, inv_radius, mode_orders):
    half_len = mode_orders.shape[0]
    return (
        jnp.concatenate(
            [mode_orders * coeffs[..., half_len:], -mode_orders * coeffs[..., :half_len]], axis=-1
        )
        * inv_radius
    )


def to_samples(rows_in, azim_table, top_mode):
    half_len = azim_table.shape[0] // 2
    if top_mode == half_len:
        return jnp.dot(rows_in, azim_table, preferred_element_type=jnp.float32)
    picked = jnp.concatenate(
        [rows_in[:, :top_mode], rows_in[:, half_len : half_len + top_mode]], axis=1
    )
    sub_table = jnp.concatenate(
        [azim_table[:top_mode], azim_table[half_len : half_len + top_mode]], axis=0
    )
    return jnp.dot(picked, sub_table, preferred_element_type=jnp.float32)


def to_modes(rows_in, azim_table, top_mode):
    half_len = azim_table.shape[0] // 2
    contract_dims = (((1,), (1,)), ((), ()))
    if top_mode == half_len:
        return lax.dot_general(
            rows_in, azim_table, contract_dims, preferred_element_type=jnp.float32
        )
    sub_table = jnp.concatenate(
        [azim_table[:top_mode], azim_table[half_len : half_len + top_mode]], axis=0
    )
    result = lax.dot_general(rows_in, sub_table, contract_dims, preferred_element_type=jnp.float32)
    filler = jnp.zeros((rows_in.shape[0], half_len - top_mode), jnp.float32)
    return jnp.concatenate([result[:, :top_mode], filler, result[:, top_mode:], filler], axis=1)


def per_device(
    disp_fwd,
    prev_fwd,
    disp_adj,
    prev_adj,
    modulus,
    radius,
    step_scale,
    kernel_in,
    buckets,
    halo_count,
    blk_nodes,
    band_nodes,
):
    derivative, quadrature = gll_tables()
    element_total = disp_fwd.shape[1]
    coeff_len = disp_fwd.shape[-1]
    mode_total = coeff_len // 2
    sample_len = modulus.shape[-1]
    azim_table = azimuth_table(mode_total)
    mode_orders = jnp.arange(mode_total, dtype=jnp.float32)
    kept_modes = mode_mask(buckets, mode_total)[:, :, None, :]
    inv_radius = 1.0 / radius[..., None]
    field_fwd = disp_fwd * kept_modes
    field_adj = disp_adj * kept_modes
    stacked = jnp.stack(
        [
            field_fwd,
            spin(field_fwd, inv_radius, mode_orders),
            field_adj,
            spin(field_adj, inv_radius, mode_orders),
        ]
    ).astype(jnp.bfloat16)
    rows_in = stacked.reshape(-1, coeff_len)
    order_tops = mode_tops(mode_total)
    highest = jnp.max(buckets)
    samples = lax.switch(
        highest,
        [partial(to_samples, top_mode=level_top) for level_top in order_tops],
        rows_in,
        azim_table,
    )
    samples = samples.reshape(4, element_total, 5, 5, sample_len)
    physical = samples[0::2]
    azimuthal = samples[1::2]
    weight = (modulus.reshape(element_total, 5, 5, sample_len) * quadrature[None, :, :, None])[None]
    grad_s = jnp.einsum("ab,febjk->feajk", derivative, physical, precision=lax.Precision.HIGHEST)
    grad_z = jnp.einsum("ab,feibk->feiak", derivative, physical, precision=lax.Precision.HIGHEST)
    diverge = jnp.einsum(
        "ba,febjk->feajk", derivative, weight * grad_s, precision=lax.Precision.HIGHEST
    ) + jnp.einsum("ba,feibk->feiak", derivative, weight * grad_z, precision=lax.Precision.HIGHEST)
    stress_phi = weight * azimuthal
    back_rows = (
        jnp.stack([diverge[0], stress_phi[0], diverge[1], stress_phi[1]])
        .astype(jnp.bfloat16)
        .reshape(-1, sample_len)
    )
    highest_back = jnp.max(buckets)
    back = lax.switch(
        highest_back,
        [partial(to_modes, top_mode=level_top) for level_top in order_tops],
        back_rows,
        azim_table,
    )
    back = back.reshape(4, 1, element_total, 25, coeff_len)
    stiff_fwd = kept_modes * (back[0] + unspin(back[1], inv_radius, mode_orders))
    stiff_adj = kept_modes * (back[2] + unspin(back[3], inv_radius, mode_orders))
    products = grad_s[0] * grad_s[1] + grad_z[0] * grad_z[1] + azimuthal[0] * azimuthal[1]
    kernel_out = kernel_in - (quadrature[None, :, :, None] * products).reshape(kernel_in.shape)
    stiff_pair = jnp.stack([stiff_fwd, stiff_adj]).reshape(2, element_total * 25, coeff_len)
    blk_lists = blk_nodes[0, 0]
    band_lists = band_nodes[0, 0]
    counts = halo_count[0, 0]
    blk_slots = jnp.arange(blk_lists.shape[1], dtype=jnp.int32)
    band_slots = jnp.arange(band_lists.shape[1], dtype=jnp.int32)
    blk_lower_send = stiff_pair[:, blk_lists[0]]
    blk_upper_send = stiff_pair[:, blk_lists[1]]
    from_below = shifted(blk_upper_send, "blk", 1)
    from_above = shifted(blk_lower_send, "blk", -1)
    band_below = shifted(stiff_pair[:, band_lists[1]], "band", 1)
    band_above = shifted(stiff_pair[:, band_lists[0]], "band", -1)
    total = stiff_pair
    total = total.at[:, blk_lists[0]].add(
        from_below * (blk_slots < counts[0]).astype(jnp.float32)[None, :, None]
    )
    total = total.at[:, blk_lists[1]].add(
        from_above * (blk_slots < counts[1]).astype(jnp.float32)[None, :, None]
    )
    total = total.at[:, band_lists[0]].add(
        band_below * (band_slots < counts[2]).astype(jnp.float32)[None, :, None]
    )
    total = total.at[:, band_lists[1]].add(
        band_above * (band_slots < counts[3]).astype(jnp.float32)[None, :, None]
    )
    total = total.reshape(2, 1, element_total, 25, coeff_len)
    growth = step_scale[..., None]
    next_fwd = kept_modes * (2.0 * field_fwd - prev_fwd - growth * total[0])
    next_adj = kept_modes * (2.0 * field_adj - prev_adj - growth * total[1])
    return (next_fwd, next_adj, kernel_out)


def solution(mesh):
    in_specs = (
        P("blk", "band", None, None),
        P("blk", "band", None, None),
        P("blk", "band", None, None),
        P("blk", "band", None, None),
        P("blk", "band", None, None),
        P("blk", "band", None),
        P("blk", "band", None),
        P("blk", "band", None, None),
        P("blk", "band"),
        P("blk", "band", None),
        P("blk", "band", None, None),
        P("blk", "band", None, None),
    )
    out_specs = (
        P("blk", "band", None, None),
        P("blk", "band", None, None),
        P("blk", "band", None, None),
    )
    return jax.shard_map(
        per_device, mesh=mesh, in_specs=in_specs, out_specs=out_specs, check_vma=False
    )
```

profile of v0, /device:TPU:25, one launch (start us, length us, event | category | flops | bytes accessed | tf_op | source)
XLA Modules:
  0.0 120.7 jit_solution(14107432445628443118)
XLA Ops:
  1.4 0.7 divide_bitcast_fusion
  2.0 1.2 convert_bitcast_fusion.1
  3.5 0.1 convert_element_type.113
  3.6 67.6 %fusion.45 = bf16[2048,2048]{1,0:T(8,128)(2,1)} fusion(s32[2048]{0:T(1024)S(1)} %fusion.80, s32[2048]{0:T(1024)S(1)} %iota_and_fusion, s32[2048]{0:T(1024)S(1)} %fusion.76, pred[2048]{0:T(1024)(128)(4,1)S(1)} %fusion.79), kind=kLoop, calls=%fused_computation.57 | loop fusion | flops 75497472 | bytes 8415232 | tf_op jit(solution)/shard_map/convert_element_type | solution.py:45
  71.2 4.8 %conditional.2 = (f32[100,2048]{1,0:T(8,128)S(1)}) conditional(s32[]{:T(128)} %bitcast.6, (bf16[100,2048]{1,0:T(8,128)(2,1)S(1)}, bf16[2048,2048]{1,0:T(8,128)(2,1)}, bf16[2048,2048]{1,0:T(8,128)(2,1)}) %tuple.32, (bf16[100,2048]{1,0:T(8,128)(2,1)S(1)}, bf16[2048,2048]{1,0:T(8,128)(2,1)}, ...), branch_computations={%region_0.1_spmd, %region_1.2_spmd, %region_2.3_spmd, %region_3.4_... | conditional | flops 838860800 | bytes 9617416 | solution.py:151
  71.2 4.8 %fusion.98 = f32[100,2048]{1,0:T(8,128)S(1)} fusion(bf16[100,2048]{1,0:T(8,128)(2,1)S(1)} %get-tuple-element.54, bf16[2048,2048]{1,0:T(8,128)(2,1)} %get-tuple-element.55), kind=kOutput, calls=%fused_computation.170 | convolution fusion | flops 838860800 | bytes 9617408 | tf_op jit(solution)/shard_map/cond/branch_3_fun/dot_general | solution.py:90
  76.2 0.7 fusion.48
  77.0 0.5 reduce
  77.5 0.9 convolution_bitcast_fusion.3
  78.5 1.4 %fusion.93 = (f32[2,1,5,5,2048]{4,2,3,0,1:T(8,128)}, bf16[2,1,5,5,2048]{4,2,3,0,1:T(8,128)(2,1)S(1)}, f32[2,5,5,2048]{3,1,2,0:T(8,128)S(1)}) fusion(f32[2,1,5,5,2048]{4,3,2,0,1:T(8,128)S(1)} %get-tuple-element.98, f32[5,5,2048]{2,0,1:T(8,128)S(1)} %copy_multiply_fusion, f32[2,5,2048,5]{2,3,1,0:T(8,128)S(1)} %fusion.48), kind=kLoop, calls=%fused_computation.165 | loop fusion | flops 307200 | bytes 2048000
  80.0 0.9 fusion.51
  80.9 0.9 fusion.47
  81.8 0.2 pad_maximum_fusion.1
  82.0 0.3 copy.72
  82.3 0.2 convert_element_type.114
  82.5 6.3 %conditional.3 = (f32[100,2048]{1,0:T(8,128)S(1)}) conditional(s32[]{:T(128)} %bitcast.6, (bf16[2048,2048]{1,0:T(8,128)(2,1)}, bf16[2048,2048]{1,0:T(8,128)(2,1)}, bf16[100,2048]{1,0:T(8,128)(2,1)S(1)}) %tuple.34, (bf16[2048,2048]{1,0:T(8,128)(2,1)}, bf16[2048,2048]{1,0:T(8,128)(2,1)}, ...), branch_computations={%region_4.5_spmd, %region_5.6_spmd, %region_6.7_spmd, %region_7.8_... | conditional | flops 838860800 | bytes 9617416 | solution.py:173
  82.7 6.1 %fusion.99 = f32[100,2048]{1,0:T(8,128)S(1)} fusion(bf16[100,2048]{1,0:T(8,128)(2,1)S(1)} %get-tuple-element.68, bf16[2048,2048]{1,0:T(8,128)(2,1)} %get-tuple-element.69), kind=kOutput, calls=%fused_computation.171 | convolution fusion | flops 838860800 | bytes 9617408 | tf_op jit(solution)/shard_map/cond/branch_3_fun/dot_general | solution.py:104
  89.0 0.1 fusion.59
  89.2 0.2 copy.73
  89.4 0.1 stack.28
  89.6 0.4 maximum_bitcast_fusion
  90.0 0.7 gather_fusion
  90.7 1.9 %collective-permute-start = (f32[2,8,2048]{2,0,1:T(2,128)S(1)}, f32[2,8,2048]{2,0,1:T(2,128)}, u32[]{:S(2)}, u32[]{:S(2)}) collective-permute-start(f32[2,8,2048]{2,0,1:T(2,128)S(1)} %bitcast.144), channel_id=1, source_target_pairs={{0,2},{2,4},{4,6},{6,8},{8,10},{10,12},{12,14},{14,16},{16,18},{18... | collective-permute-start | bytes 393224 | tf_op jit(solution)/shard_map/ppermute | solution.py:14
  92.6 0.7 gather_fusion.1
  93.3 5.2 %collective-permute-start.1 = (f32[2,8,2048]{2,0,1:T(2,128)S(1)}, f32[2,8,2048]{2,0,1:T(2,128)S(1)}, u32[]{:S(2)}, u32[]{:S(2)}) collective-permute-start(f32[2,8,2048]{2,0,1:T(2,128)S(1)} %bitcast.143), channel_id=1, source_target_pairs={{2,0},{4,2},{6,4},{8,6},{10,8},{12,10},{14,12},{16,14},{18,16},{20... | collective-permute-start | bytes 393224 | tf_op jit(solution)/shard_map/ppermute | solution.py:14
  98.5 0.6 gather_fusion.2
  99.1 1.3 %collective-permute-start.2 = (f32[2,4,2048]{2,0,1:T(2,128)S(1)}, f32[2,4,2048]{2,0,1:T(2,128)}, u32[]{:S(2)}, u32[]{:S(2)}) collective-permute-start(f32[2,4,2048]{2,0,1:T(2,128)S(1)} %bitcast.148), channel_id=1, source_target_pairs={{0,1},{2,3},{4,5},{6,7},{8,9},{10,11},{12,13},{14,15},{16,17},{18,... | collective-permute-start | bytes 196616 | tf_op jit(solution)/shard_map/ppermute | solution.py:14
  100.4 1.2 %gather_fusion.3 = f32[4,2,2048]{2,1,0:T(2,128)} fusion(f32[2,25,2048]{2,0,1:T(2,128)S(1)} %maximum_bitcast_fusion, s32[1024]{0:T(1024)S(1)} %get-tuple-element.144), kind=kCustom, calls=%fused_computation.3 | custom fusion | bytes 131088 | tf_op jit(solution)/shard_map/gather | solution.py:195
  101.7 3.6 %collective-permute-start.3 = (f32[2,4,2048]{2,0,1:T(2,128)}, f32[2,4,2048]{2,0,1:T(2,128)S(1)}, u32[]{:S(2)}, u32[]{:S(2)}) collective-permute-start(f32[2,4,2048]{2,0,1:T(2,128)} %bitcast.55), channel_id=1, source_target_pairs={{1,0},{3,2},{5,4},{7,6},{9,8},{11,10},{13,12},{15,14},{17,16},{19,... | collective-permute-start | bytes 196616 | tf_op jit(solution)/shard_map/ppermute | solution.py:14
  105.3 0.3 copy.132
  105.6 1.2 fusion.54
  106.7 0.2 copy.77
  107.0 0.6 fusion.97
  107.6 0.6 compare_convert_fusion.3
  108.2 0.7 compare_convert_fusion.2
  108.9 0.6 compare_convert_fusion.1
  109.5 1.6 %multiply_subtract_fusion = f32[1,1,25,2048]{3,1,2,0:T(1,128)} fusion(f32[1,1,25,2048]{3,1,2,0:T(1,128)S(1)} %copy-done.3, f32[1,1,25,2048]{3,1,2,0:T(1,128)S(1)} %bitcast.142, f32[25]{0:T(128)} %constant.91), kind=kLoop, calls=%fused_computation.107 | loop fusion | flops 102400 | bytes 614500 | tf_op jit(solution)/shard_map/sub | solution.py:183
  111.1 0.6 compare_convert_fusion
  111.8 0.9 multiply_bitcast_fusion.4
  112.8 1.0 multiply_bitcast_fusion.2
  113.8 1.0 scatter_fusion
  114.9 1.0 scatter_fusion.1
  115.9 0.7 scatter_fusion.2
  116.7 0.7 scatter_fusion.3
  117.4 0.3 fusion.94
  117.8 1.2 fusion.64
  118.9 0.9 copy.78
  119.8 0.9 copy.79
  (50 shorter events, 1.1 us)
Async XLA Ops:
  71.2 5.1 %copy-start.6 = (f32[5,5,1,1]{1,0,3,2:T(8,128)S(1)}, f32[5,5,1,1]{1,0,3,2:T(8,128)}, u32[]{:S(2)}) copy-start(f32[5,5,1,1]{1,0,3,2:T(8,128)} %constant.92) | copy-start | bytes 304
  71.2 5.8 %copy-start.2 = (f32[1,1,25,2048]{3,1,2,0:T(1,128)S(1)}, f32[1,1,25,2048]{3,1,2,0:T(1,128)}, u32[]{:S(2)}) copy-start(f32[1,1,25,2048]{3,1,2,0:T(1,128)} %param.26) | copy-start | bytes 614404
  76.0 2.4 %copy-start.8 = (f32[5,5]{0,1:T(8,128)S(1)}, f32[5,5]{0,1:T(8,128)}, u32[]{:S(2)}) copy-start(f32[5,5]{0,1:T(8,128)} %constant.78.clone) | copy-start | bytes 304
  82.5 7.0 %copy-start.9 = (s32[1,1,2,8]{3,2,1,0:T(2,128)S(1)}, s32[1,1,2,8]{3,2,1,0:T(2,128)}, u32[]{:S(2)}) copy-start(s32[1,1,2,8]{3,2,1,0:T(2,128)} %param.32) | copy-start | bytes 196
  82.5 15.9 %copy-start.10 = (s32[1,1,2,4]{3,2,1,0:T(2,128)S(1)}, s32[1,1,2,4]{3,2,1,0:T(2,128)}, u32[]{:S(2)}) copy-start(s32[1,1,2,4]{3,2,1,0:T(2,128)} %param.33) | copy-start | bytes 100
  88.9 18.1 %copy-start.7 = (s32[1,1,4]{2,1,0:T(1,128)S(1)}, s32[1,1,4]{2,1,0:T(1,128)}, u32[]{:S(2)}) copy-start(s32[1,1,4]{2,1,0:T(1,128)} %param.31) | copy-start | bytes 52
  88.9 20.6 %copy-start.3 = (f32[1,1,25,2048]{3,1,2,0:T(1,128)S(1)}, f32[1,1,25,2048]{3,1,2,0:T(1,128)}, u32[]{:S(2)}) copy-start(f32[1,1,25,2048]{3,1,2,0:T(1,128)} %param.29) | copy-start | bytes 614404
  88.9 28.9 %copy-start = (f32[1,1,25,2048]{3,1,2,0:T(1,128)S(1)}, f32[1,1,25,2048]{3,1,2,0:T(1,128)}, u32[]{:S(2)}) copy-start(f32[1,1,25,2048]{3,1,2,0:T(1,128)} %param.22) | copy-start | bytes 614404
  88.9 28.8 %copy-start.1 = (f32[1,1,25,2048]{3,1,2,0:T(1,128)S(1)}, f32[1,1,25,2048]{3,1,2,0:T(1,128)}, u32[]{:S(2)}) copy-start(f32[1,1,25,2048]{3,1,2,0:T(1,128)} %param.24) | copy-start | bytes 614404
  88.9 28.8 %copy-start.4 = (f32[1,1,25,2048]{3,1,2,0:T(1,128)S(1)}, f32[1,1,25,2048]{3,1,2,0:T(1,128)}, u32[]{:S(2)}) copy-start(f32[1,1,25,2048]{3,1,2,0:T(1,128)} %param.25) | copy-start | bytes 614404
  88.9 28.8 %copy-start.5 = (f32[1,1,25,2048]{3,1,2,0:T(1,128)S(1)}, f32[1,1,25,2048]{3,1,2,0:T(1,128)}, u32[]{:S(2)}) copy-start(f32[1,1,25,2048]{3,1,2,0:T(1,128)} %param.23) | copy-start | bytes 614404
  90.7 22.1 %collective-permute-start = (f32[2,8,2048]{2,0,1:T(2,128)S(1)}, f32[2,8,2048]{2,0,1:T(2,128)}, u32[]{:S(2)}, u32[]{:S(2)}) collective-permute-start(f32[2,8,2048]{2,0,1:T(2,128)S(1)} %bitcast.144), channel_id=1, source_target_pairs={{0,2},{2,4},{4,6},{6,8},{8,10},{10,12},{12,14},{14,16},{16,18},{18... | collective-permute-start | bytes 393224 | tf_op jit(solution)/shard_map/ppermute | solution.py:14
  93.3 21.5 %collective-permute-start.1 = (f32[2,8,2048]{2,0,1:T(2,128)S(1)}, f32[2,8,2048]{2,0,1:T(2,128)S(1)}, u32[]{:S(2)}, u32[]{:S(2)}) collective-permute-start(f32[2,8,2048]{2,0,1:T(2,128)S(1)} %bitcast.143), channel_id=1, source_target_pairs={{2,0},{4,2},{6,4},{8,6},{10,8},{12,10},{14,12},{16,14},{18,16},{20... | collective-permute-start | bytes 393224 | tf_op jit(solution)/shard_map/ppermute | solution.py:14
  99.1 12.6 %collective-permute-start.2 = (f32[2,4,2048]{2,0,1:T(2,128)S(1)}, f32[2,4,2048]{2,0,1:T(2,128)}, u32[]{:S(2)}, u32[]{:S(2)}) collective-permute-start(f32[2,4,2048]{2,0,1:T(2,128)S(1)} %bitcast.148), channel_id=1, source_target_pairs={{0,1},{2,3},{4,5},{6,7},{8,9},{10,11},{12,13},{14,15},{16,17},{18,... | collective-permute-start | bytes 196616 | tf_op jit(solution)/shard_map/ppermute | solution.py:14
  101.7 11.0 %collective-permute-start.3 = (f32[2,4,2048]{2,0,1:T(2,128)}, f32[2,4,2048]{2,0,1:T(2,128)S(1)}, u32[]{:S(2)}, u32[]{:S(2)}) collective-permute-start(f32[2,4,2048]{2,0,1:T(2,128)} %bitcast.55), channel_id=1, source_target_pairs={{1,0},{3,2},{5,4},{7,6},{9,8},{11,10},{13,12},{15,14},{17,16},{19,... | collective-permute-start | bytes 196616 | tf_op jit(solution)/shard_map/ppermute | solution.py:14
where the time goes:
time: 121 us
  other arithmetic  84.5 us (70%)
  matrix products  14.3 us (12%)
  starting transfers between devices  12 us (10%)
  local copies, waits for them, and re-layouts  7.8 us (6%)
  between operations  1.91 us (2%)
    convert_element_type x1, other arithmetic, azimuth_table(): (jnp.cos(phase.astype(jnp.float32) * (2.0 * math.pi / sample_len)) * fact...  67.6 us
    ppermute x4, starting transfers between devices, shifted(): lax.ppermute(value, axis, [(source, source + steps) for source in range(i...  12 us
    dot_general x1, matrix products, to_modes(): lax.dot_general(rows_in, azim_table, contract_dims, preferred_element_typ...  6.11 us
    dot_general x1, matrix products, to_samples(): return jnp.dot(rows_in, azim_table, preferred_element_type=jnp.float32)  4.77 us
  transfers between devices with their start and end apart: 4, of which 0 were waited for; matrix products, arithmetic and copies ran while one was open for 10% of the time, Pallas kernels for 0%

commit v1 on v0

v1 whole, which is shorter than its diff:
```python
import functools
import math

import jax
import jax.numpy as jnp
import ml_dtypes
import numpy as np
from jax import lax
from jax.experimental import pallas as pl
from jax.experimental.pallas import tpu as pltpu
from jax.sharding import PartitionSpec as P

MESH = pl.DeviceIdType.MESH


def gll_tables():
    inner_root = math.sqrt(3.0 / 7.0)
    points = np.array([-1.0, -inner_root, 0.0, inner_root, 1.0])
    weights = np.array([0.1, 49.0 / 90.0, 32.0 / 45.0, 49.0 / 90.0, 0.1])
    legendre = (35.0 * points**4 - 30.0 * points**2 + 3.0) / 8.0
    derivative = np.zeros((5, 5))
    for target in range(5):
        for source in range(5):
            if target != source:
                derivative[target, source] = (
                    legendre[target] / legendre[source] / (points[target] - points[source])
                )
    derivative[0, 0] = -5.0
    derivative[4, 4] = 5.0
    return derivative.astype(np.float32), np.outer(weights, weights).astype(np.float32)


def half_table(mode_total, width):
    sample_len = 2 * mode_total
    rows = np.arange(2 * mode_total, dtype=np.int64)
    quarter = (rows >= mode_total) * (sample_len // 4)
    phase = ((rows % mode_total)[:, None] * np.arange(mode_total)[None] + quarter[:, None]) % sample_len
    levels = np.cos(np.arange(sample_len) * (2.0 * math.pi / sample_len)) * math.sqrt(2.0 / sample_len)
    levels = levels.astype(np.float32).astype(ml_dtypes.bfloat16)
    table = levels[phase]
    return table.reshape(2 * mode_total, mode_total // width, width).transpose(1, 0, 2)


def split_bf16(value):
    high = value.astype(np.float32).astype(ml_dtypes.bfloat16)
    low = (value.astype(np.float32) - high.astype(np.float32)).astype(ml_dtypes.bfloat16)
    return high, low


def node_operators(pad):
    derivative, quadrature = gll_tables()
    eye = np.eye(5, dtype=np.float32)
    along_s = np.zeros((pad, pad), np.float32)
    along_z = np.zeros((pad, pad), np.float32)
    along_s[:25, :25] = np.kron(derivative, eye)
    along_z[:25, :25] = np.kron(eye, derivative)
    grad_hi, grad_lo = split_bf16(np.concatenate([along_s, along_z], axis=0))
    div_hi, div_lo = split_bf16(np.concatenate([along_s.T, along_z.T], axis=1))
    quad = np.zeros((pad, 128), np.float32)
    quad[:25] = quadrature.reshape(25, 1)
    return (
        np.concatenate([grad_hi, grad_hi, grad_lo], axis=1),
        np.concatenate([div_hi, div_hi, div_lo], axis=1),
        quad,
    )


def halves(value):
    high = value.astype(jnp.bfloat16)
    low = (value - high.astype(jnp.float32)).astype(jnp.bfloat16)
    return high, low


def mm(lhs, rhs):
    return jnp.dot(lhs, rhs, preferred_element_type=jnp.float32)


def padded(value, pad):
    extra = pad - value.shape[0]
    return jnp.concatenate([value, jnp.zeros((extra, value.shape[1]), value.dtype)], axis=0)


def column_of(row, pad):
    count = row.shape[1]
    sub = lax.broadcasted_iota(jnp.int32, (pad, count), 0)
    lane = lax.broadcasted_iota(jnp.int32, (pad, count), 1)
    return jnp.sum(jnp.where(sub == lane, row, 0.0), axis=1, keepdims=True)


def kernel(
    blk_total,
    band_total,
    nodes,
    pad,
    width,
    disp_fwd,
    prev_fwd,
    disp_adj,
    prev_adj,
    modulus,
    kernel_in,
    radius,
    step_scale,
    grad_op,
    div_op,
    quad,
    bucket,
    counts,
    blk_nodes,
    band_nodes,
    table_hbm,
    next_fwd,
    next_adj,
    kernel_out,
    table,
    rows,
    low,
    stiff,
    send_blk,
    send_band,
    recv_blk,
    recv_band,
    table_sem,
    send_sem,
    recv_sem,
):
    blk = lax.axis_index("blk")
    band = lax.axis_index("band")
    half = disp_fwd.shape[-1] // 2
    chunks = half // width
    blk_slots = blk_nodes.shape[-1]
    band_slots = band_nodes.shape[-1]
    links = [
        (blk > 0, (blk - 1, band)),
        (blk < blk_total - 1, (blk + 1, band)),
        (band > 0, (blk, band - 1)),
        (band < band_total - 1, (blk, band + 1)),
    ]
    loads = [
        pltpu.make_async_copy(table_hbm.at[c], table.at[c], table_sem.at[c]) for c in range(chunks)
    ]
    for load in loads:
        load.start()
    barrier = pltpu.get_barrier_semaphore()
    for here, peer in links:

        @pl.when(here)
        def _():
            pl.semaphore_signal(barrier, inc=1, device_id=peer, device_id_type=MESH)

    def landing(c, side):
        return recv_blk.at[c, side] if side < 2 else recv_band.at[c, side - 2]

    def leaving(c, side):
        return send_blk.at[c, side] if side < 2 else send_band.at[c, side - 2]

    def transfer(c, side):
        return pltpu.make_async_remote_copy(
            src_ref=leaving(c, side),
            dst_ref=landing(c, side ^ 1),
            send_sem=send_sem.at[c, side],
            recv_sem=recv_sem.at[c, side ^ 1],
            device_id=links[side][1],
            device_id_type=MESH,
        )

    def arrival(c, side):
        return pltpu.make_async_remote_copy(
            src_ref=leaving(c, side),
            dst_ref=landing(c, side),
            send_sem=send_sem.at[c, side],
            recv_sem=recv_sem.at[c, side],
            device_id=links[side][1],
            device_id_type=MESH,
        )

    for side in range(4):

        @pl.when(jnp.logical_not(links[side][0]))
        def _():
            for c in range(chunks):
                ref = landing(c, side)
                ref[...] = jnp.zeros(ref.shape, ref.dtype)

    level = bucket[0, 0]
    tops = [max(half // 64, 1), max(half // 16, 1), max(half // 4, 1), half]
    limit = jnp.where(
        level == 0, tops[0], jnp.where(level == 1, tops[1], jnp.where(level == 2, tops[2], tops[3]))
    )
    radius_col = column_of(radius[0], pad)
    sub_col = lax.broadcasted_iota(jnp.int32, (pad, 1), 0)
    inv_radius = jnp.where(sub_col < nodes, 1.0 / radius_col, 0.0)
    growth = column_of(step_scale[0], pad)
    quad_col = quad[:, 0:1]
    fields = ((disp_fwd, prev_fwd, next_fwd), (disp_adj, prev_adj, next_adj))

    def orders(c):
        m = lax.broadcasted_iota(jnp.int32, (1, width), 1) + c * width
        kept = (m < limit).astype(jnp.float32)
        sign = (1 - 2 * (m % 2)).astype(jnp.float32)
        return m.astype(jnp.float32), kept, sign

    for f, (disp, _, _) in enumerate(fields):
        for c in range(chunks):
            m, kept, sign = orders(c)
            re_cols = slice(c * width, (c + 1) * width)
            im_cols = slice(half + c * width, half + (c + 1) * width)
            real = padded(disp[0, 0, :, re_cols], pad) * kept
            imag = padded(disp[0, 0, :, im_cols], pad) * kept
            spin_re = -m * imag * inv_radius
            spin_im = m * real * inv_radius
            for k, (re_part, im_part) in enumerate(((real, imag), (spin_re, spin_im))):
                at = (4 * f + 2 * k) * pad
                rows[at : at + pad, re_cols] = re_part.astype(jnp.bfloat16)
                rows[at : at + pad, im_cols] = im_part.astype(jnp.bfloat16)
                rows[at + pad : at + 2 * pad, re_cols] = (re_part * sign).astype(jnp.bfloat16)
                rows[at + pad : at + 2 * pad, im_cols] = (im_part * sign).astype(jnp.bfloat16)

    for c in range(chunks):
        loads[c].wait()
        samples = mm(rows[...], table[c])
        chunk_cols = slice(c * width, (c + 1) * width)
        for h in range(2):
            cols = slice(h * half + c * width, h * half + (c + 1) * width)
            weight = padded(modulus[0, 0, :, cols], pad) * quad_col
            terms = []
            for f in range(2):
                at = (4 * f + h) * pad
                physical = samples[at : at + pad]
                azimuthal = samples[at + 2 * pad : at + 3 * pad]
                high, lower = halves(physical)
                grads = mm(grad_op[...], jnp.concatenate([high, lower, high], axis=0))
                grad_s, grad_z = grads[:pad], grads[pad:]
                high_s, low_s = halves(weight * grad_s)
                high_z, low_z = halves(weight * grad_z)
                diverge = mm(
                    div_op[...],
                    jnp.concatenate([high_s, high_z, low_s, low_z, high_s, high_z], axis=0),
                )
                low[at : at + pad, chunk_cols] = diverge.astype(jnp.bfloat16)
                low[at + 2 * pad : at + 3 * pad, chunk_cols] = (weight * azimuthal).astype(
                    jnp.bfloat16
                )
                terms.append((grad_s, grad_z, azimuthal))
            product = sum(one * two for one, two in zip(*terms))
            kernel_out[0, 0, :, cols] = kernel_in[0, 0, :, cols] - (quad_col * product)[:nodes]

    pl.semaphore_wait(barrier, sum(here.astype(jnp.int32) for here, _ in links))

    for c in range(chunks):
        m, kept, sign = orders(c)
        cosines = mm(low[...], table[c, :half])
        sines = mm(low[...], table[c, half:])

        def joined(result, group):
            at = group * pad
            return result[at : at + pad] + sign * result[at + pad : at + 2 * pad]

        for f in range(2):
            real = kept * (joined(cosines, 4 * f) + m * joined(sines, 4 * f + 2) * inv_radius)
            imag = kept * (joined(sines, 4 * f) - m * joined(cosines, 4 * f + 2) * inv_radius)
            stiff[c, f, :, :width] = real
            stiff[c, f, :, width:] = imag
        for side in range(2):
            for f in range(2):
                for s in range(blk_slots):
                    node = blk_nodes[0, 0, side, s]
                    at = f * blk_slots + s
                    send_blk[c, side, at : at + 1, :] = stiff[c, f, pl.ds(node, 1), :]
                for s in range(band_slots):
                    node = band_nodes[0, 0, side, s]
                    at = f * band_slots + s
                    send_band[c, side, at : at + 1, :] = stiff[c, f, pl.ds(node, 1), :]
        for side in range(4):

            @pl.when(links[side][0])
            def _():
                transfer(c, side).start()

    slot_rows = 4 * (blk_slots + band_slots)
    lane = lax.broadcasted_iota(jnp.int32, (1, 2 * slot_rows), 1) % slot_rows
    target = jnp.full((1, 2 * slot_rows), -1, jnp.int32)
    at = 0
    for side in range(4):
        lists = blk_nodes if side < 2 else band_nodes
        for f in range(2):
            for s in range(lists.shape[-1]):
                node = jnp.where(s < counts[0, 0, side], lists[0, 0, side % 2, s] + f * pad, -1)
                target = jnp.where(lane == at, node, target)
                at += 1
    sub = lax.broadcasted_iota(jnp.int32, (2 * pad, 2 * slot_rows), 0)
    placer = jnp.where(sub == target, 1.0, 0.0).astype(jnp.bfloat16)

    for c in range(chunks):
        for side in range(4):

            @pl.when(links[side][0])
            def _():
                arrival(c, side).wait_recv()

        m, kept, _ = orders(c)
        arrived = jnp.concatenate([landing(c, side)[...] for side in range(4)], axis=0)
        high, lower = halves(arrived)
        placed = mm(placer, jnp.concatenate([high, lower], axis=0))
        for f, (disp, prev, out) in enumerate(fields):
            for part in range(2):
                cols = slice(part * half + c * width, part * half + (c + 1) * width)
                sect = slice(part * width, (part + 1) * width)
                total = stiff[c, f, :, sect] + placed[f * pad : (f + 1) * pad, sect]
                out[0, 0, :, cols] = kept * (
                    2.0 * disp[0, 0, :, cols] - prev[0, 0, :, cols] - (growth * total)[:nodes]
                )
    for c in range(chunks):
        for side in range(4):

            @pl.when(links[side][0])
            def _():
                transfer(c, side).wait_send()


def per_device(
    blk_total,
    band_total,
    disp_fwd,
    prev_fwd,
    disp_adj,
    prev_adj,
    modulus,
    radius,
    step_scale,
    kernel_in,
    buckets,
    halo_count,
    blk_nodes,
    band_nodes,
):
    nodes, coeff_len = disp_fwd.shape[2:]
    half = coeff_len // 2
    width = min(512, half)
    chunks = half // width
    pad = -(-nodes // 16) * 16
    blk_slots = blk_nodes.shape[-1]
    band_slots = band_nodes.shape[-1]
    grad_op, div_op, quad = node_operators(pad)
    table = half_table(half, width)
    vmem = pl.BlockSpec(memory_space=pltpu.VMEM)
    smem = pl.BlockSpec(memory_space=pltpu.SMEM)
    out = jax.ShapeDtypeStruct(disp_fwd.shape, jnp.float32)
    return pl.pallas_call(
        functools.partial(kernel, blk_total, band_total, nodes, pad, width),
        out_shape=(out, out, out),
        in_specs=[vmem] * 11 + [smem] * 4 + [pl.BlockSpec(memory_space=pltpu.HBM)],
        out_specs=(vmem, vmem, vmem),
        scratch_shapes=[
            pltpu.VMEM(table.shape, jnp.bfloat16),
            pltpu.VMEM((8 * pad, coeff_len), jnp.bfloat16),
            pltpu.VMEM((8 * pad, half), jnp.bfloat16),
            pltpu.VMEM((chunks, 2, pad, 2 * width), jnp.float32),
            pltpu.VMEM((chunks, 2, 2 * blk_slots, 2 * width), jnp.float32),
            pltpu.VMEM((chunks, 2, 2 * band_slots, 2 * width), jnp.float32),
            pltpu.VMEM((chunks, 2, 2 * blk_slots, 2 * width), jnp.float32),
            pltpu.VMEM((chunks, 2, 2 * band_slots, 2 * width), jnp.float32),
            pltpu.SemaphoreType.DMA((chunks,)),
            pltpu.SemaphoreType.DMA((chunks, 4)),
            pltpu.SemaphoreType.DMA((chunks, 4)),
        ],
        compiler_params=pltpu.CompilerParams(
            collective_id=0, has_side_effects=True, vmem_limit_bytes=60 * 1024 * 1024
        ),
    )(
        disp_fwd,
        prev_fwd,
        disp_adj,
        prev_adj,
        modulus,
        kernel_in,
        radius,
        step_scale,
        jnp.asarray(grad_op),
        jnp.asarray(div_op),
        jnp.asarray(quad),
        buckets,
        halo_count,
        blk_nodes,
        band_nodes,
        jnp.asarray(table),
    )


def solution(mesh):
    wide = P("blk", "band", None, None)
    line = P("blk", "band", None)
    in_specs = (wide,) * 5 + (line, line, wide, P("blk", "band"), line, wide, wide)
    return jax.shard_map(
        functools.partial(per_device, mesh.shape["blk"], mesh.shape["band"]),
        mesh=mesh,
        in_specs=in_specs,
        out_specs=(wide,) * 3,
        check_vma=False,
    )
```

time: 121 us -> 34 us (0.28)
  the two profiles are of different devices: /device:TPU:25 before, /device:TPU:0 now
where the time goes in v1:
time: 34 us; the launch traced here: 33.6 us
  Pallas kernels  16.6 us (49%)
  local copies, waits for them, and re-layouts  15.7 us (46%)
  between operations  1.29 us (4%)
    pallas_call x1, Pallas kernels, per_device(): pl.pallas_call(functools.partial(kernel, blk_total, band_total, nodes, pa...  16.6 us
    unnamed x6, local copies, waits for them, and re-layouts  10.2 us
    pallas_call x3, local copies, waits for them, and re-layouts, per_device(): pl.pallas_call(functools.partial(kernel, blk_total, band_total, nodes, pa...  5.52 us

profile of v1, /device:TPU:0, one launch (start us, length us, event | category | flops | bytes accessed | tf_op | source)
XLA Modules:
  0.0 33.6 jit_solution(13546116620055421473)
XLA Ops:
  1.3 1.7 %copy.19.disp_fwd = f32[1,1,25,2048]{3,2,1,0:T(8,128)} copy(f32[1,1,25,2048]{3,1,2,0:T(1,128)} %param.16) | data formatting | bytes 409600 | tf_op args[0]
  3.0 1.7 %copy.20.prev_fwd = f32[1,1,25,2048]{3,2,1,0:T(8,128)} copy(f32[1,1,25,2048]{3,1,2,0:T(1,128)} %param.17) | data formatting | bytes 409600 | tf_op args[1]
  4.7 1.7 %copy.21.disp_adj = f32[1,1,25,2048]{3,2,1,0:T(8,128)} copy(f32[1,1,25,2048]{3,1,2,0:T(1,128)} %param.18) | data formatting | bytes 409600 | tf_op args[2]
  6.4 1.7 %copy.22.prev_adj = f32[1,1,25,2048]{3,2,1,0:T(8,128)} copy(f32[1,1,25,2048]{3,1,2,0:T(1,128)} %param.19) | data formatting | bytes 409600 | tf_op args[3]
  8.1 1.7 %copy.23.modulus = f32[1,1,25,2048]{3,2,1,0:T(8,128)} copy(f32[1,1,25,2048]{3,1,2,0:T(1,128)} %param.20) | data formatting | bytes 409600 | tf_op args[4]
  9.8 1.7 %copy.24.kernel_in = f32[1,1,25,2048]{3,2,1,0:T(8,128)} copy(f32[1,1,25,2048]{3,1,2,0:T(1,128)} %param.23) | data formatting | bytes 409600 | tf_op args[7]
  11.5 16.6 %shard_map.175 = (f32[1,1,25,2048]{3,2,1,0:T(8,128)}, f32[1,1,25,2048]{3,2,1,0:T(8,128)}, f32[1,1,25,2048]{3,2,1,0:T(8,128)}) custom-call(f32[1,1,25,2048]{3,2,1,0:T(8,128)} %copy.19.disp_fwd, f32[1,1,25,2048]{3,2,1,0:T(8,128)} %copy.20.prev_fwd, f32[1,1,25,2048]{3,2,1,0:T(8,128)} %copy.21.disp_adj, f32[1,1,25,2048]{3,2,1,0:T(8,128)} %copy.22.prev_adj, ...), custom_call_target="tpu_custom_call" | custom-call | tf_op jit(solution)/shard_map/pallas_call | solution.py:349
  28.1 1.8 %copy.25 = f32[1,1,25,2048]{3,1,2,0:T(1,128)} copy(f32[1,1,25,2048]{3,2,1,0:T(8,128)} %get-tuple-element.3) | data formatting | bytes 409600 | tf_op jit(solution)/shard_map/pallas_call | solution.py:349
  29.9 1.8 %copy.26 = f32[1,1,25,2048]{3,1,2,0:T(1,128)} copy(f32[1,1,25,2048]{3,2,1,0:T(8,128)} %get-tuple-element.4) | data formatting | bytes 409600 | tf_op jit(solution)/shard_map/pallas_call | solution.py:349
  31.8 1.8 %copy.27 = f32[1,1,25,2048]{3,1,2,0:T(1,128)} copy(f32[1,1,25,2048]{3,2,1,0:T(8,128)} %get-tuple-element.5) | data formatting | bytes 409600 | tf_op jit(solution)/shard_map/pallas_call | solution.py:349

commit v2 on v1

--- a/solution.py
+++ b/solution.py
@@ -80,6 +80,19 @@
     return jnp.concatenate([value, jnp.zeros((extra, value.shape[1]), value.dtype)], axis=0)
 
 
+def take(ref, nodes, start, size):
+    stride = ref.shape[0] // nodes
+    return jnp.concatenate(
+        [ref[pl.ds(start // 128 + j, nodes, stride=stride), :] for j in range(size // 128)], axis=1
+    )
+
+
+def put(ref, nodes, start, value):
+    stride = ref.shape[0] // nodes
+    for j in range(value.shape[1] // 128):
+        ref[pl.ds(start // 128 + j, nodes, stride=stride), :] = value[:, j * 128 : (j + 1) * 128]
+
+
 def column_of(row, pad):
     count = row.shape[1]
     sub = lax.broadcasted_iota(jnp.int32, (pad, count), 0)
@@ -93,25 +106,35 @@
     nodes,
     pad,
     width,
-    disp_fwd,
-    prev_fwd,
-    disp_adj,
-    prev_adj,
-    modulus,
-    kernel_in,
-    radius,
-    step_scale,
-    grad_op,
-    div_op,
-    quad,
-    bucket,
-    counts,
-    blk_nodes,
-    band_nodes,
+    disp_fwd_hbm,
+    prev_fwd_hbm,
+    disp_adj_hbm,
+    prev_adj_hbm,
+    modulus_hbm,
+    kernel_in_hbm,
+    radius_hbm,
+    step_hbm,
+    bucket_hbm,
+    grad_hbm,
+    div_hbm,
+    quad_hbm,
+    counts_hbm,
+    blk_nodes_hbm,
+    band_nodes_hbm,
     table_hbm,
     next_fwd,
     next_adj,
     kernel_out,
+    held,
+    radius,
+    step_scale,
+    bucket,
+    grad_op,
+    div_op,
+    quad,
+    counts,
+    blk_nodes,
+    band_nodes,
     table,
     rows,
     low,
@@ -120,13 +143,41 @@
     send_band,
     recv_blk,
     recv_band,
+    held_sem,
+    small_sem,
     table_sem,
     send_sem,
     recv_sem,
 ):
+    disp_fwd, disp_adj, modulus, kernel_in, prev_fwd, prev_adj = (held.at[i] for i in range(6))
+    sources = (disp_fwd_hbm, disp_adj_hbm, modulus_hbm, kernel_in_hbm, prev_fwd_hbm, prev_adj_hbm)
+    fetches = [
+        pltpu.make_async_copy(source, held.at[i], held_sem.at[i])
+        for i, source in enumerate(sources)
+    ]
+    small = [
+        pltpu.make_async_copy(source, target, small_sem.at[i])
+        for i, (source, target) in enumerate(
+            (
+                (radius_hbm, radius),
+                (step_hbm, step_scale),
+                (bucket_hbm, bucket),
+                (grad_hbm, grad_op),
+                (div_hbm, div_op),
+                (quad_hbm, quad),
+                (counts_hbm, counts),
+                (blk_nodes_hbm, blk_nodes),
+                (band_nodes_hbm, band_nodes),
+            )
+        )
+    ]
+    fetches[0].start()
+    for copy in small:
+        copy.start()
+    fetches[1].start()
     blk = lax.axis_index("blk")
     band = lax.axis_index("band")
-    half = disp_fwd.shape[-1] // 2
+    half = disp_fwd_hbm.shape[0] // nodes * 128 // 2
     chunks = half // width
     blk_slots = blk_nodes.shape[-1]
     band_slots = band_nodes.shape[-1]
@@ -141,6 +192,8 @@
     ]
     for load in loads:
         load.start()
+    for fetch in fetches[2:]:
+        fetch.start()
     barrier = pltpu.get_barrier_semaphore()
     for here, peer in links:
 
@@ -182,7 +235,9 @@
                 ref = landing(c, side)
                 ref[...] = jnp.zeros(ref.shape, ref.dtype)
 
-    level = bucket[0, 0]
+    for copy in small:
+        copy.wait()
+    level = bucket[...]
     tops = [max(half // 64, 1), max(half // 16, 1), max(half // 4, 1), half]
     limit = jnp.where(
         level == 0, tops[0], jnp.where(level == 1, tops[1], jnp.where(level == 2, tops[2], tops[3]))
@@ -201,12 +256,13 @@
         return m.astype(jnp.float32), kept, sign
 
     for f, (disp, _, _) in enumerate(fields):
+        fetches[f].wait()
         for c in range(chunks):
             m, kept, sign = orders(c)
             re_cols = slice(c * width, (c + 1) * width)
             im_cols = slice(half + c * width, half + (c + 1) * width)
-            real = padded(disp[0, 0, :, re_cols], pad) * kept
-            imag = padded(disp[0, 0, :, im_cols], pad) * kept
+            real = padded(take(disp, nodes, c * width, width), pad) * kept
+            imag = padded(take(disp, nodes, half + c * width, width), pad) * kept
             spin_re = -m * imag * inv_radius
             spin_im = m * real * inv_radius
             for k, (re_part, im_part) in enumerate(((real, imag), (spin_re, spin_im))):
@@ -218,11 +274,14 @@
 
     for c in range(chunks):
         loads[c].wait()
+        if c == 0:
+            fetches[2].wait()
+            fetches[3].wait()
         samples = mm(rows[...], table[c])
         chunk_cols = slice(c * width, (c + 1) * width)
         for h in range(2):
-            cols = slice(h * half + c * width, h * half + (c + 1) * width)
-            weight = padded(modulus[0, 0, :, cols], pad) * quad_col
+            start = h * half + c * width
+            weight = padded(take(modulus, nodes, start, width), pad) * quad_col
             terms = []
             for f in range(2):
                 at = (4 * f + h) * pad
@@ -243,7 +302,8 @@
                 )
                 terms.append((grad_s, grad_z, azimuthal))
             product = sum(one * two for one, two in zip(*terms))
-            kernel_out[0, 0, :, cols] = kernel_in[0, 0, :, cols] - (quad_col * product)[:nodes]
+            change = (quad_col * product)[:nodes]
+            put(kernel_out, nodes, start, take(kernel_in, nodes, start, width) - change)
 
     pl.semaphore_wait(barrier, sum(here.astype(jnp.int32) for here, _ in links))
 
@@ -291,6 +351,8 @@
     sub = lax.broadcasted_iota(jnp.int32, (2 * pad, 2 * slot_rows), 0)
     placer = jnp.where(sub == target, 1.0, 0.0).astype(jnp.bfloat16)
 
+    fetches[4].wait()
+    fetches[5].wait()
     for c in range(chunks):
         for side in range(4):
 
@@ -304,18 +366,28 @@
         placed = mm(placer, jnp.concatenate([high, lower], axis=0))
         for f, (disp, prev, out) in enumerate(fields):
             for part in range(2):
-                cols = slice(part * half + c * width, part * half + (c + 1) * width)
+                start = part * half + c * width
+                now, before = (take(ref, nodes, start, width) for ref in (disp, prev))
                 sect = slice(part * width, (part + 1) * width)
                 total = stiff[c, f, :, sect] + placed[f * pad : (f + 1) * pad, sect]
-                out[0, 0, :, cols] = kept * (
-                    2.0 * disp[0, 0, :, cols] - prev[0, 0, :, cols] - (growth * total)[:nodes]
-                )
+                put(out, nodes, start, kept * (2.0 * now - before - (growth * total)[:nodes]))
     for c in range(chunks):
         for side in range(4):
 
             @pl.when(links[side][0])
             def _():
                 transfer(c, side).wait_send()
+
+
+def deliver(one, two, three, one_out, two_out, three_out, sems):
+    copies = [
+        pltpu.make_async_copy(source, target, sems.at[i])
+        for i, (source, target) in enumerate(((one, one_out), (two, two_out), (three, three_out)))
+    ]
+    for copy in copies:
+        copy.start()
+    for copy in copies:
+        copy.wait()
 
 
 def per_device(
@@ -343,15 +415,26 @@
     band_slots = band_nodes.shape[-1]
     grad_op, div_op, quad = node_operators(pad)
     table = half_table(half, width)
-    vmem = pl.BlockSpec(memory_space=pltpu.VMEM)
-    smem = pl.BlockSpec(memory_space=pltpu.SMEM)
-    out = jax.ShapeDtypeStruct(disp_fwd.shape, jnp.float32)
-    return pl.pallas_call(
+    anywhere = pl.BlockSpec(memory_space=pl.ANY)
+    hbm = pl.BlockSpec(memory_space=pltpu.HBM)
+    flat = (nodes * coeff_len // 128, 128)
+    out = jax.ShapeDtypeStruct(flat, jnp.float32)
+    outs = pl.pallas_call(
         functools.partial(kernel, blk_total, band_total, nodes, pad, width),
-        out_shape=(out, out, out),
-        in_specs=[vmem] * 11 + [smem] * 4 + [pl.BlockSpec(memory_space=pltpu.HBM)],
-        out_specs=(vmem, vmem, vmem),
+        out_shape=(pltpu.VMEM(flat, jnp.float32),) * 3,
+        in_specs=[hbm] * 16,
+        out_specs=(pl.BlockSpec(memory_space=pltpu.VMEM),) * 3,
         scratch_shapes=[
+            pltpu.VMEM((6, *flat), jnp.float32),
+            pltpu.VMEM(radius.shape, jnp.float32),
+            pltpu.VMEM(step_scale.shape, jnp.float32),
+            pltpu.VMEM(buckets.shape, jnp.int32),
+            pltpu.VMEM(grad_op.shape, jnp.bfloat16),
+            pltpu.VMEM(div_op.shape, jnp.bfloat16),
+            pltpu.VMEM(quad.shape, jnp.float32),
+            pltpu.SMEM(halo_count.shape, jnp.int32),
+            pltpu.SMEM(blk_nodes.shape, jnp.int32),
+            pltpu.SMEM(band_nodes.shape, jnp.int32),
             pltpu.VMEM(table.shape, jnp.bfloat16),
             pltpu.VMEM((8 * pad, coeff_len), jnp.bfloat16),
             pltpu.VMEM((8 * pad, half), jnp.bfloat16),
@@ -360,31 +443,42 @@
             pltpu.VMEM((chunks, 2, 2 * band_slots, 2 * width), jnp.float32),
             pltpu.VMEM((chunks, 2, 2 * blk_slots, 2 * width), jnp.float32),
             pltpu.VMEM((chunks, 2, 2 * band_slots, 2 * width), jnp.float32),
+            pltpu.SemaphoreType.DMA((6,)),
+            pltpu.SemaphoreType.DMA((9,)),
             pltpu.SemaphoreType.DMA((chunks,)),
             pltpu.SemaphoreType.DMA((chunks, 4)),
             pltpu.SemaphoreType.DMA((chunks, 4)),
         ],
         compiler_params=pltpu.CompilerParams(
-            collective_id=0, has_side_effects=True, vmem_limit_bytes=60 * 1024 * 1024
+            collective_id=0, has_side_effects=True, vmem_limit_bytes=67043328 - 3 * 4 * nodes * coeff_len - 40 * 1024
         ),
     )(
-        disp_fwd,
-        prev_fwd,
-        disp_adj,
-        prev_adj,
-        modulus,
-        kernel_in,
+        disp_fwd.reshape(flat),
+        prev_fwd.reshape(flat),
+        disp_adj.reshape(flat),
+        prev_adj.reshape(flat),
+        modulus.reshape(flat),
+        kernel_in.reshape(flat),
         radius,
         step_scale,
+        buckets,
         jnp.asarray(grad_op),
         jnp.asarray(div_op),
         jnp.asarray(quad),
-        buckets,
         halo_count,
         blk_nodes,
         band_nodes,
         jnp.asarray(table),
     )
+    outs = pl.pallas_call(
+        deliver,
+        out_shape=(out, out, out),
+        in_specs=[pl.BlockSpec(memory_space=pltpu.VMEM)] * 3,
+        out_specs=(hbm,) * 3,
+        scratch_shapes=[pltpu.SemaphoreType.DMA((3,))],
+        compiler_params=pltpu.CompilerParams(vmem_limit_bytes=4 * 1024 * 1024),
+    )(*outs)
+    return tuple(value.reshape(disp_fwd.shape) for value in outs)
 
 
 def solution(mesh):

time: 34 us -> 17.2 us (0.51)
  local copies, waits for them, and re-layouts: 15.7 us -> 0 us
  Pallas kernels: 16.6 us -> 15.8 us
    unnamed x6 -> x0, local copies, waits for them, and re-layouts: 10.2 us -> none
    pallas_call x3 -> x0, local copies, waits for them, and re-layouts: 5.52 us -> none  [per_device(): pl.pallas_call(functools.partial(kernel, blk_total, band_total, nodes, pa...]
    pallas_call x1, Pallas kernels: 16.6 us -> 14.9 us  [per_device(): pl.pallas_call(functools.partial(kernel, blk_total, band_total, nodes, pa...]
    pallas_call x0 -> x1, Pallas kernels: none -> 0.84 us  [per_device(): pl.pallas_call(deliver, out_shape=(out, out, out), in_specs=[pl.BlockSpec...]
where the time goes in v2:
time: 17.2 us; the launch traced here: 17.1 us
  Pallas kernels  15.8 us (92%)
  between operations  1.29 us (8%)
    pallas_call x1, Pallas kernels, per_device(): pl.pallas_call(functools.partial(kernel, blk_total, band_total, nodes, pa...  14.9 us
    pallas_call x1, Pallas kernels, per_device(): pl.pallas_call(deliver, out_shape=(out, out, out), in_specs=[pl.BlockSpec...  0.84 us

profile of v2, /device:TPU:0, one launch (start us, length us, event | category | flops | bytes accessed | tf_op | source)
XLA Modules:
  0.0 17.1 jit_solution(15862382482845022011)
XLA Ops:
  1.3 14.9 %shard_map.175 = (f32[400,128]{1,0:T(8,128)S(1)}, f32[400,128]{1,0:T(8,128)S(1)}, f32[400,128]{1,0:T(8,128)S(1)}) custom-call(f32[400,128]{1,0:T(8,128)} %bitcast.9, f32[400,128]{1,0:T(8,128)} %bitcast.10, f32[400,128]{1,0:T(8,128)} %bitcast.11, f32[400,128]{1,0:T(8,128)} %bitcast.12, f32[400,128]{1,0:T(8,128)} %bitcast.13, f32[400,128]{1,0:T(8,128)} %bitcast.14, ...), custom_call_target="tpu_custom_call" | custom-call | tf_op jit(solution)/shard_map/pallas_call | solution.py:422
  16.2 0.8 %shard_map.176 = (f32[400,128]{1,0:T(8,128)}, f32[400,128]{1,0:T(8,128)}, f32[400,128]{1,0:T(8,128)}) custom-call(f32[400,128]{1,0:T(8,128)S(1)} %get-tuple-element.9.one, f32[400,128]{1,0:T(8,128)S(1)} %get-tuple-element.10.two, f32[400,128]{1,0:T(8,128)S(1)} %get-tuple-element.11.three), custom_call_target="tpu_custom_call" | custom-call | tf_op jit(solution)/shard_map/pallas_call | solution.py:473
